TPU v7x, 32 devices: a whole 2x2x4 slice. The times are simulated.
32 devices in a mesh: dp: 4 (over z), expert: 2 (over x), shard: 4 (over y, core).
Axes of the slice: x: 2, y: 2, z: 4, core: 2. Of those that a mesh axis runs over, the one named last changes fastest.
Arguments:
- activations: bfloat16 [2, 2, 2048, 256], P(None, 'expert', ('dp', 'shard')), may hold values from -6 to 6
- out_grads: bfloat16 [2, 2, 2048, 14336], P(None, 'expert', ('dp', 'shard')), may hold values from -0.25 to 0.25
- weights: float32 [2, 2, 256, 14336], P(None, 'expert', ('dp', 'shard')), may hold values from -4 to 4
- shadow: float32 [2, 2, 256, 14336], P(None, 'expert', ('dp', 'shard')), may hold values from -4 to 4
- counts: int32 [2, 32, 2], P(None, ('dp', 'expert', 'shard')), may hold values from 1 to 1024, as said below
Outputs:
- new_weights: float32 [2, 2, 256, 14336], P(None, 'expert', ('dp', 'shard'))
- new_shadow: float32 [2, 2, 256, 14336], P(None, 'expert', ('dp', 'shard'))
Inputs may be any that keep to these rules, and one draw needn't show every extreme that they name: `counts`: loads differ between the experts of a layer.
All inputs are finite; a program needn't handle non-finite values.
Results may differ from a plain program's by a relative error of at most 0.0003.
Values sent between devices are 32-bit elements; how exact they have to be, the bound alone decides.
No kernel may reach another device: no remote copies, remote signals or barrier semaphores. Data moves between devices by JAX's collectives and lax.ppermute only.
A program may use at most 128 MiB of HBM per device.

v0:
```python
from functools import partial

import jax
import jax.numpy as jnp
from jax import lax
from jax.sharding import PartitionSpec as P

LAYERS = 2


step_size = 0.5
clip_level = 1.0


def partial_rows(inputs, cotangent, start, count):
    return lax.dot_general(
        inputs, cotangent, (((0,), (0,)), ((), ())), preferred_element_type=jnp.float32
    )


def on_device(activations, out_grads, weights, shadow, counts):
    experts = counts.shape[-1]
    own_slot = (jnp.arange(experts) == lax.axis_index("expert")).astype(jnp.float32)
    own_rows = weights.shape[2]
    load_totals = lax.psum(counts[:, 0, :], ("dp", "expert", "shard"))
    all_weights = []
    all_shadow = []
    for layer_index in range(LAYERS):
        inputs = activations[layer_index, 0]
        cotangent = out_grads[layer_index, 0]
        term = partial(partial_rows, inputs, cotangent)
        summed = lax.psum_scatter(
            term(jnp.int32(0), lax.axis_size(("dp", "shard")) * own_rows),
            ("dp", "shard"),
            scatter_dimension=0,
            tiled=True,
        )
        squares = jnp.sum(summed * summed)
        loads = load_totals[layer_index].astype(jnp.float32)
        total_squares = lax.psum(squares, ("dp", "shard"))
        own_load = jnp.sum(loads * own_slot)
        mean_load = jnp.mean(loads)
        numel = inputs.shape[1] * cotangent.shape[1]
        root_mean = jnp.sqrt(total_squares / numel)
        factor = (
            step_size * (own_load / mean_load) * clip_level / jnp.maximum(root_mean, clip_level)
        )
        updated = weights[layer_index, 0] - factor * summed
        beta = own_load / (own_load + mean_load)
        previous = shadow[layer_index, 0]
        all_weights.append(updated)
        all_shadow.append(previous + beta * (updated - previous))
    return (jnp.stack(all_weights)[:, None], jnp.stack(all_shadow)[:, None])


def solution(mesh):
    in_specs = (
        P(None, "expert", ("dp", "shard"), None),
        P(None, "expert", ("dp", "shard"), None),
        P(None, "expert", ("dp", "shard"), None),
        P(None, "expert", ("dp", "shard"), None),
        P(None, ("dp", "expert", "shard"), None),
    )
    out_specs = (P(None, "expert", ("dp", "shard"), None), P(None, "expert", ("dp", "shard"), None))
    return jax.shard_map(
        on_device, mesh=mesh, in_specs=in_specs, out_specs=out_specs, check_vma=False
    )
```

profile of v0, /device:TPU:0, one launch (start us, length us, event | category | flops | bytes accessed | tf_op | source)
XLA Modules:
  0.0 370.9 jit_solution(8719449823756068406)
XLA Ops:
  7.2 0.0 reduce-scatter.5.cloned.1.call-start
  7.2 9.4 %fusion = f32[256,14336]{1,0:T(8,128)} fusion(bf16[2,1,128,14336]{3,2,1,0:T(8,128)(2,1)} %param.6, bf16[2,1,128,256]{3,2,1,0:T(8,128)(2,1)} %param.5), kind=kOutput, calls=%fused_computation | convolution fusion | flops 939524096 | bytes 18415616 | tf_op jit(solution)/shard_map/dot_general | solution.py:16
  16.6 0.0 copy-start.1
  16.6 0.0 reduce-scatter.5.cloned.1.call-update
  16.6 0.0 reduce-scatter.3.cloned.1.call-start
  16.7 0.8 copy-done.1
  17.5 10.1 %fusion.2 = f32[256,14336]{1,0:T(8,128)} fusion(bf16[2,1,128,14336]{3,2,1,0:T(8,128)(2,1)} %param.6, bf16[2,1,128,256]{3,2,1,0:T(8,128)(2,1)S(1)} %copy-done.1), kind=kOutput, calls=%fused_computation.2 | convolution fusion | flops 939524096 | bytes 18415616 | tf_op jit(solution)/shard_map/dot_general | solution.py:16
  27.6 0.0 copy-start.2
  27.6 0.0 copy-start
  27.6 0.0 reduce-scatter.3.cloned.1.call-update
  27.7 0.7 copy-done.2
  28.3 46.0 %psum.21 = s32[2,2]{1,0:T(2,128)S(1)} all-reduce(s32[2,2]{1,0:T(2,128)S(1)} %bitcast.63), channel_id=1, replica_groups=mesh['dp'=4,'expert'=2,'shard'=4] {'dp','expert','shard'}, use_global_device_ids=true, to_apply=%region_0.0 | all-reduce | flops 4 | bytes 32 | tf_op jit(solution)/shard_map/psum | solution.py:25
  74.3 0.7 convert_reduce_fusion.1
  75.7 0.6 fusion.16
  80.2 89.7 %reduce-scatter.5.cloned.1.call-done = f32[16,14336]{1,0:T(8,128)} async-done(((f32[256,14336]{1,0:T(8,128)}), f32[16,14336]{1,0:T(8,128)}) %reduce-scatter.5.cloned.1.call-update) | async-done | bytes 917520 | tf_op jit(solution)/shard_map/reduce_scatter | solution.py:32
  169.9 2.0 multiply_reduce_fusion
  171.9 151.3 %reduce-scatter.3.cloned.1.call-done = f32[16,14336]{1,0:T(8,128)} async-done(((f32[256,14336]{1,0:T(8,128)}), f32[16,14336]{1,0:T(8,128)}) %reduce-scatter.3.cloned.1.call-update) | async-done | bytes 917520 | tf_op jit(solution)/shard_map/reduce_scatter | solution.py:32
  323.2 2.1 multiply_reduce_fusion.1
  325.9 32.2 %all-reduce = (f32[]{:T(128)}, f32[]{:T(128)}) all-reduce(f32[]{:T(128)} %multiply_reduce_fusion, f32[]{:T(128)} %multiply_reduce_fusion.1), channel_id=1, replica_groups=mesh['dp'=4,'expert'=2,'shard'=4] {'dp','shard'}, use_global_device_ids=true, to_apply=%region_10.0 | all-reduce | flops 2 | bytes 16 | tf_op jit(solution)/shard_map/psum | solution.py:40
  359.6 0.0 copy-done
  359.6 2.4 fusion.9
  362.0 2.1 maximum_bitcast_fusion
Async XLA Ops:
  7.2 162.7 %reduce-scatter.5.cloned.1.call-start = ((), (), s32[]{:S(2)}) async-start(), calls=%async_computation.3 | async-start | bytes 15597568 | tf_op jit(solution)/shard_map/reduce_scatter | solution.py:32
  16.6 0.9 copy-start.1
  16.6 306.6 %reduce-scatter.3.cloned.1.call-start = ((), (), s32[]{:S(2)}) async-start(), calls=%async_computation.2 | async-start | bytes 15597568 | tf_op jit(solution)/shard_map/reduce_scatter | solution.py:32
  27.6 0.7 copy-start.2
  27.6 332.0 %copy-start = (f32[2,1,16,14336]{3,2,1,0:T(8,128)S(1)}, f32[2,1,16,14336]{3,2,1,0:T(8,128)}, u32[]{:S(2)}) copy-start(f32[2,1,16,14336]{3,2,1,0:T(8,128)} %param.8) | copy-start | bytes 5505028
Sparse Core Ops, SparseCore 0:
  16.8 153.1 reduce-scatter.4
  174.0 149.1 reduce-scatter.2
where the time goes:
time: 371 us
  waiting for transfers between devices  241 us (65%)
  blocking collectives  78.2 us (21%)
  between operations  20.8 us (6%)
  matrix products  19.5 us (5%)
  other arithmetic  9.86 us (3%)
    reduce_scatter x2, waiting for transfers between devices, on_device(): lax.psum_scatter(term(jnp.int32(0), lax.axis_size(('dp', 'shard')) * own_...  241 us
    psum x1, blocking collectives, on_device(): load_totals = lax.psum(counts[:, 0, :], ('dp', 'expert', 'shard'))  46 us
    psum x1, blocking collectives, on_device(): total_squares = lax.psum(squares, ('dp', 'shard'))  32.2 us
    dot_general x2, matrix products, partial_rows(): lax.dot_general(inputs, cotangent, (((0,), (0,)), ((), ())), preferred_el...  19.5 us
  transfers between devices with their start and end apart: 2, of which 2 were waited for; matrix products, arithmetic and copies ran while one was open for 4% of the time, Pallas kernels for 0%

commit v1 on v0

v1 whole, which is shorter than its diff:
```python
import jax
import jax.numpy as jnp
from jax import lax
from jax.sharding import PartitionSpec as P


GROUP = ("dp", "shard")
CHUNKS = 4
step_size = 0.5
clip_level = 1.0


def bits_of(size):
    return [1 << k for k in range(size.bit_length() - 1)]


def swap(value, size, bit):
    return lax.ppermute(value, GROUP, [(g, g ^ bit) for g in range(size)])


def summed_over(value, axis):
    size = lax.axis_size(axis)
    total = value
    for bit in bits_of(size):
        total = total + lax.ppermute(total, axis, [(g, g ^ bit) for g in range(size)])
    return total


def relative_rows(inputs, order, own_rows, me):
    rows = inputs.shape[1]
    position = lax.broadcasted_iota(jnp.int32, (rows, rows), 0)
    block = position // own_rows
    relative = jnp.zeros_like(block)
    for place, bit in enumerate(reversed(order)):
        relative = relative + ((block >> place) & 1) * bit
    source = (relative ^ me) * own_rows + position % own_rows
    pick = (source == lax.broadcasted_iota(jnp.int32, (rows, rows), 1)).astype(inputs.dtype)
    return lax.dot_general(
        pick, inputs, (((1,), (1,)), ((), ())), preferred_element_type=jnp.float32
    ).astype(inputs.dtype)


def issue_order(jobs, links, own_rows, size):
    now, done, free, arrival, stage = 0.0, [], {}, [0.0] * len(jobs), [0] * len(jobs)
    while len(done) < sum(len(order) + 1 for order, _ in jobs):
        open_jobs = [j for j in range(len(jobs)) if stage[j] <= len(jobs[j][0])]
        begun = [j for j in open_jobs if stage[j] > 0 and arrival[j] <= now]
        fresh = [j for j in open_jobs if stage[j] == 0]
        if begun:
            job = min(begun, key=lambda j: arrival[j])
        elif fresh:
            job = fresh[0]
        else:
            job = min(open_jobs, key=lambda j: arrival[j])
            now = arrival[job]
        order, width = jobs[job]
        at = stage[job]
        now += 2.5
        if at < len(order):
            link = links[order[at]]
            rate = 6e5 if link == "core" else 5e4
            sent = (size >> (at + 1)) * own_rows * width * 4 / rate
            free[link] = max(free.get(link, 0.0), now) + sent
            arrival[job] = free[link] + 2.0
        done.append((job, at))
        stage[job] += 1
    return done


def reduce_all(jobs, links, lefts, rights, own_rows, size):
    arrived = [[] for _ in jobs]
    results = [None] * len(jobs)
    waiting = None

    def settle(job, at, value):
        order = jobs[job][0]
        if at < len(order):
            arrived[job].append(swap(value, size, order[at]))
        else:
            results[job] = value

    for job, at in issue_order(jobs, links, own_rows, size):
        left = lefts[job]
        if waiting is not None:
            before, step, value = waiting
            left, value = lax.optimization_barrier((left, value))
            settle(before, step, value)
        low = 0 if at == len(jobs[job][0]) else (size >> (at + 1)) * own_rows
        high = (size >> at) * own_rows
        value = lax.dot_general(
            left[low:high],
            rights[job],
            (((1,), (0,)), ((), ())),
            preferred_element_type=jnp.float32,
        )
        for got in arrived[job]:
            value = value + got[low:high]
        waiting = (job, at, value)
    settle(*waiting)
    return results


def exchange_order(dp, shard):
    shard_bits = bits_of(shard)
    dp_bits = [bit * shard for bit in bits_of(dp)]
    first, rest = shard_bits[:1], shard_bits[1:]
    links = {bit: "dp" for bit in dp_bits} | {bit: "shard" for bit in rest}
    links |= {bit: "core" for bit in first}
    plain = first + rest + dp_bits
    early = first + dp_bits[:1] + rest + dp_bits[1:]
    return links, plain, early


def all_jobs(layers, columns, plain, early):
    width = columns // CHUNKS
    return [(early if chunk == 1 else plain, width) for _ in range(layers) for chunk in range(CHUNKS)]


def on_device(activations, out_grads, weights, shadow, counts):
    layers, _, _, columns = out_grads.shape
    experts = counts.shape[-1]
    own_rows = weights.shape[2]
    size = lax.axis_size(GROUP)
    me = lax.axis_index(GROUP)
    links, plain, early = exchange_order(lax.axis_size("dp"), lax.axis_size("shard"))
    jobs = all_jobs(layers, columns, plain, early)
    own_slot = (jnp.arange(experts) == lax.axis_index("expert")).astype(jnp.float32)
    load_sums = summed_over(counts[:, 0, :].astype(jnp.float32), "expert")

    width = columns // CHUNKS
    lefts, rights = [], []
    for layer in range(layers):
        inputs = activations[layer, 0]
        rows_of = {}
        for order in (plain, early):
            rows_of[tuple(order)] = relative_rows(inputs, order, own_rows, me)
        for chunk in range(CHUNKS):
            order = early if chunk == 1 else plain
            lefts.append(rows_of[tuple(order)])
            rights.append(out_grads[layer, 0, :, chunk * width : (chunk + 1) * width])
    pieces = reduce_all(jobs, links, lefts, rights, own_rows, size)
    grads = [pieces[layer * CHUNKS : (layer + 1) * CHUNKS] for layer in range(layers)]
    squares = jnp.stack([sum(jnp.sum(piece * piece) for piece in layer) for layer in grads])
    totals = jnp.concatenate([load_sums.reshape(-1), squares])
    for axis in ("shard", "dp"):
        totals = summed_over(totals, axis)
    load_totals = totals[: layers * experts].reshape(layers, experts)
    total_squares = totals[layers * experts :]

    all_weights, all_shadow = [], []
    for layer in range(layers):
        loads = load_totals[layer]
        own_load = jnp.sum(loads * own_slot)
        mean_load = jnp.mean(loads)
        root_mean = jnp.sqrt(total_squares[layer] / (own_rows * size * columns))
        factor = (
            step_size * (own_load / mean_load) * clip_level / jnp.maximum(root_mean, clip_level)
        )
        beta = own_load / (own_load + mean_load)
        summed = jnp.concatenate(grads[layer], axis=1)
        updated = weights[layer, 0] - factor * summed
        previous = shadow[layer, 0]
        all_weights.append(updated)
        all_shadow.append(previous + beta * (updated - previous))
    return (jnp.stack(all_weights)[:, None], jnp.stack(all_shadow)[:, None])


def solution(mesh):
    split = P(None, "expert", ("dp", "shard"), None)
    in_specs = (split, split, split, split, P(None, ("dp", "expert", "shard"), None))

    def step(activations, out_grads, weights, shadow, counts):
        return jax.shard_map(
            on_device, mesh=mesh, in_specs=in_specs, out_specs=(split, split), check_vma=False
        )(activations, out_grads, weights, shadow, counts)

    return step
```

time: 371 us -> 260 us (0.70)
  waiting for transfers between devices: 241 us -> 139 us
  blocking collectives: 78.2 us -> 0 us
  starting transfers between devices: 0.08 us -> 39.6 us
  matrix products: 19.5 us -> 54.1 us
  between operations: 20.8 us -> 12.8 us
    reduce_scatter x2 -> x0, waiting for transfers between devices: 241 us -> none  [on_device(): lax.psum_scatter(term(jnp.int32(0), lax.axis_size(('dp', 'shard')) * own_...]
    ppermute x0 -> x37, waiting for transfers between devices: none -> 139 us  [the longest x32 126 us: swap(): return lax.ppermute(value, GROUP, [(g, g ^ bit) for g in range(size)])]
    psum x2 -> x0, blocking collectives: 78.2 us -> none  [the longest x1 46 us: on_device(): load_totals = lax.psum(counts[:, 0, :], ('dp', 'expert', 'shard'))]
    ppermute x0 -> x37, starting transfers between devices: none -> 39.6 us  [the longest x32 34.9 us: swap(): return lax.ppermute(value, GROUP, [(g, g ^ bit) for g in range(size)])]
    dot_general x2 -> x44, matrix products: 19.5 us -> 54.1 us  [the longest x40 50.3 us: reduce_all(): lax.dot_general(left[low:high], rights[job], (((1,), (0,)), ((), ())), pr...]
  transfers between devices with their start and end apart: 2 -> 37, of which waited for: 2 -> 22; matrix products, arithmetic and copies ran while one was open for 4% -> 19% of each run, Pallas kernels for 0% -> 0%
where the time goes in v1:
time: 260 us; the launch traced here: 259 us
  waiting for transfers between devices  139 us (53%)
  matrix products  54.1 us (21%)
  starting transfers between devices  39.6 us (15%)
  between operations  12.8 us (5%)
  other arithmetic  11.9 us (5%)
    ppermute x32, waiting for transfers between devices, swap(): return lax.ppermute(value, GROUP, [(g, g ^ bit) for g in range(size)])  126 us
    dot_general x40, matrix products, reduce_all(): lax.dot_general(left[low:high], rights[job], (((1,), (0,)), ((), ())), pr...  50.3 us
    ppermute x32, starting transfers between devices, swap(): return lax.ppermute(value, GROUP, [(g, g ^ bit) for g in range(size)])  34.9 us
    ppermute x5, waiting for transfers between devices, summed_over(): lax.ppermute(total, axis, [(g, g ^ bit) for g in range(size)])  12.5 us
    reduce_sum x7, other arithmetic, on_device(): jnp.sum(piece * piece)  5.72 us
  transfers between devices with their start and end apart: 37, of which 22 were waited for; matrix products, arithmetic and copies ran while one was open for 19% of the time, Pallas kernels for 0%

profile of v1, /device:TPU:0, one launch (start us, length us, event | category | flops | bytes accessed | tf_op | source)
XLA Modules:
  0.0 258.6 jit_solution(6272990084482356933)
XLA Ops:
  26.1 2.9 %collective-permute-start = (f32[2,2]{1,0:T(2,128)S(1)}, f32[2,2]{1,0:T(2,128)S(1)}, u32[]{:S(2)}, u32[]{:S(2)}) collective-permute-start(f32[2,2]{1,0:T(2,128)S(1)} %bitcast.213), channel_id=1, source_target_pairs={{0,4},{4,0},{1,5},{5,1},{2,6},{6,2},{3,7},{7,3},{8,12},{12,8},{9,1... | collective-permute-start | bytes 56 | tf_op jit(solution)/shard_map/ppermute | solution.py:25
  34.3 2.4 slice_add_fusion.3
  38.5 15.6 %collective-permute-done.7 = f32[64,3584]{1,0:T(8,128)} collective-permute-done((f32[64,3584]{1,0:T(8,128)}, f32[64,3584]{1,0:T(8,128)}, u32[]{:S(2)}, u32[]{:S(2)}) %collective-permute-start.7) | collective-permute-done | bytes 917536 | tf_op jit(solution)/shard_map/ppermute | solution.py:18
  63.5 29.8 %collective-permute-done.11 = f32[64,3584]{1,0:T(8,128)S(1)} collective-permute-done((f32[64,3584]{1,0:T(8,128)}, f32[64,3584]{1,0:T(8,128)S(1)}, u32[]{:S(2)}, u32[]{:S(2)}) %collective-permute-start.11) | collective-permute-done | bytes 917536 | tf_op jit(solution)/shard_map/ppermute | solution.py:18
  101.1 2.7 %collective-permute-start.16 = (f32[16,3584]{1,0:T(8,128)S(1)}, f32[16,3584]{1,0:T(8,128)S(1)}, u32[]{:S(2)}, u32[]{:S(2)}) collective-permute-start(f32[16,3584]{1,0:T(8,128)S(1)} %slice_add_fusion.69), channel_id=1, source_target_pairs={{0,16},{1,17},{2,18},{3,19},{8,24},{9,25},{10,26},{11,27},{16,0},{... | collective-permute-start | bytes 688136 | tf_op jit(solution)/shard_map/ppermute | solution.py:18
  104.0 5.5 %collective-permute-done.15 = f32[32,3584]{1,0:T(8,128)S(1)} collective-permute-done((f32[32,3584]{1,0:T(8,128)S(1)}, f32[32,3584]{1,0:T(8,128)S(1)}, u32[]{:S(2)}, u32[]{:S(2)}) %collective-permute-start.15) | collective-permute-done | bytes 458784 | tf_op jit(solution)/shard_map/ppermute | solution.py:18
  113.3 7.2 %collective-permute-done.17 = f32[32,3584]{1,0:T(8,128)S(1)} collective-permute-done((f32[32,3584]{1,0:T(8,128)S(1)}, f32[32,3584]{1,0:T(8,128)S(1)}, u32[]{:S(2)}, u32[]{:S(2)}) %collective-permute-start.17) | collective-permute-done | bytes 458784 | tf_op jit(solution)/shard_map/ppermute | solution.py:18
  120.4 3.7 %collective-permute-start.19 = (f32[16,3584]{1,0:T(8,128)S(1)}, f32[16,3584]{1,0:T(8,128)S(1)}, u32[]{:S(2)}, u32[]{:S(2)}) collective-permute-start(f32[16,3584]{1,0:T(8,128)S(1)} %slice_add_fusion.66), channel_id=1, source_target_pairs={{0,16},{1,17},{2,18},{3,19},{8,24},{9,25},{10,26},{11,27},{16,0},{... | collective-permute-start | bytes 688136 | tf_op jit(solution)/shard_map/ppermute | solution.py:18
  124.3 18.1 %collective-permute-done.18 = f32[64,3584]{1,0:T(8,128)S(1)} collective-permute-done((f32[64,3584]{1,0:T(8,128)S(1)}, f32[64,3584]{1,0:T(8,128)S(1)}, u32[]{:S(2)}, u32[]{:S(2)}) %collective-permute-start.18) | collective-permute-done | bytes 917536 | tf_op jit(solution)/shard_map/ppermute | solution.py:18
  142.4 3.1 %collective-permute-start.20 = (f32[16,3584]{1,0:T(8,128)S(1)}, f32[16,3584]{1,0:T(8,128)S(1)}, u32[]{:S(2)}, u32[]{:S(2)}) collective-permute-start(f32[16,3584]{1,0:T(8,128)S(1)} %slice_add_fusion.60), channel_id=1, source_target_pairs={{0,16},{1,17},{2,18},{3,19},{8,24},{9,25},{10,26},{11,27},{16,0},{... | collective-permute-start | bytes 688136 | tf_op jit(solution)/shard_map/ppermute | solution.py:18
  149.4 2.3 collective-permute-done.20
  154.8 4.5 %collective-permute-done.21 = f32[32,3584]{1,0:T(8,128)S(1)} collective-permute-done((f32[32,3584]{1,0:T(8,128)S(1)}, f32[32,3584]{1,0:T(8,128)S(1)}, u32[]{:S(2)}, u32[]{:S(2)}) %collective-permute-start.21) | collective-permute-done | bytes 458784 | tf_op jit(solution)/shard_map/ppermute | solution.py:18
  165.5 5.9 %collective-permute-done.23 = f32[16,3584]{1,0:T(8,128)S(1)} collective-permute-done((f32[16,3584]{1,0:T(8,128)S(1)}, f32[16,3584]{1,0:T(8,128)S(1)}, u32[]{:S(2)}, u32[]{:S(2)}) %collective-permute-start.23) | collective-permute-done | bytes 229408 | tf_op jit(solution)/shard_map/ppermute | solution.py:18
  174.3 4.3 %collective-permute-done.25 = f32[32,3584]{1,0:T(8,128)S(1)} collective-permute-done((f32[32,3584]{1,0:T(8,128)S(1)}, f32[32,3584]{1,0:T(8,128)S(1)}, u32[]{:S(2)}, u32[]{:S(2)}) %collective-permute-start.25) | collective-permute-done | bytes 458784 | tf_op jit(solution)/shard_map/ppermute | solution.py:18
  180.7 11.1 %collective-permute-done.26 = f32[16,3584]{1,0:T(8,128)S(1)} collective-permute-done((f32[16,3584]{1,0:T(8,128)S(1)}, f32[16,3584]{1,0:T(8,128)S(1)}, u32[]{:S(2)}, u32[]{:S(2)}) %collective-permute-start.26) | collective-permute-done | bytes 229408 | tf_op jit(solution)/shard_map/ppermute | solution.py:18
  192.9 3.0 %collective-permute-done.27 = f32[16,3584]{1,0:T(8,128)S(1)} collective-permute-done((f32[16,3584]{1,0:T(8,128)S(1)}, f32[16,3584]{1,0:T(8,128)S(1)}, u32[]{:S(2)}, u32[]{:S(2)}) %collective-permute-start.27) | collective-permute-done | bytes 229408 | tf_op jit(solution)/shard_map/ppermute | solution.py:18
  197.8 2.4 slice_add_fusion.8
  204.9 2.5 collective-permute-start.31
  209.0 7.9 %collective-permute-done.30 = f32[32,3584]{1,0:T(8,128)S(1)} collective-permute-done((f32[32,3584]{1,0:T(8,128)}, f32[32,3584]{1,0:T(8,128)S(1)}, u32[]{:S(2)}, u32[]{:S(2)}) %collective-permute-start.30) | collective-permute-done | bytes 458784 | tf_op jit(solution)/shard_map/ppermute | solution.py:18
  222.7 6.9 %collective-permute-done.32 = f32[16,3584]{1,0:T(8,128)S(1)} collective-permute-done((f32[16,3584]{1,0:T(8,128)S(1)}, f32[16,3584]{1,0:T(8,128)S(1)}, u32[]{:S(2)}, u32[]{:S(2)}) %collective-permute-start.32) | collective-permute-done | bytes 229408 | tf_op jit(solution)/shard_map/ppermute | solution.py:18
  235.1 2.2 collective-permute-done.34
  237.3 3.6 %collective-permute-done.35 = f32[6]{0:T(128)S(1)} collective-permute-done((f32[6]{0:T(128)S(1)}, f32[6]{0:T(128)S(1)}, u32[]{:S(2)}, u32[]{:S(2)}) %collective-permute-start.35) | collective-permute-done | bytes 56 | tf_op jit(solution)/shard_map/ppermute | solution.py:25
  241.4 4.0 %collective-permute-done.36 = f32[6]{0:T(128)S(1)} collective-permute-done((f32[6]{0:T(128)S(1)}, f32[6]{0:T(128)S(1)}, u32[]{:S(2)}, u32[]{:S(2)}) %collective-permute-start.36) | collective-permute-done | bytes 56 | tf_op jit(solution)/shard_map/ppermute | solution.py:25
  253.4 2.5 bitcast_add_fusion.1
  (162 shorter events, 91.9 us)
Async XLA Ops:
  20.2 12.5 %collective-permute-start.5 = (f32[128,3584]{1,0:T(8,128)}, f32[128,3584]{1,0:T(8,128)}, u32[]{:S(2)}, u32[]{:S(2)}) collective-permute-start(f32[128,3584]{1,0:T(8,128)} %fusion.48), channel_id=1, source_target_pairs={{0,1},{1,0},{2,3},{3,2},{8,9},{9,8},{10,11},{11,10},{16,17},{17,16... | collective-permute-start | bytes 5505032 | tf_op jit(solution)/shard_map/ppermute | solution.py:18
  22.2 14.5 %collective-permute-start.6 = (f32[128,3584]{1,0:T(8,128)}, f32[128,3584]{1,0:T(8,128)}, u32[]{:S(2)}, u32[]{:S(2)}) collective-permute-start(f32[128,3584]{1,0:T(8,128)} %fusion.36), channel_id=1, source_target_pairs={{0,1},{1,0},{2,3},{3,2},{8,9},{9,8},{10,11},{11,10},{16,17},{17,16... | collective-permute-start | bytes 5505032 | tf_op jit(solution)/shard_map/ppermute | solution.py:18
  24.0 33.8 %collective-permute-start.8 = (f32[128,3584]{1,0:T(8,128)}, f32[128,3584]{1,0:T(8,128)}, u32[]{:S(2)}, u32[]{:S(2)}) collective-permute-start(f32[128,3584]{1,0:T(8,128)} %fusion.24), channel_id=1, source_target_pairs={{0,1},{1,0},{2,3},{3,2},{8,9},{9,8},{10,11},{11,10},{16,17},{17,16... | collective-permute-start | bytes 5505032 | tf_op jit(solution)/shard_map/ppermute | solution.py:18
  26.0 35.8 %collective-permute-start.10 = (f32[128,3584]{1,0:T(8,128)}, f32[128,3584]{1,0:T(8,128)}, u32[]{:S(2)}, u32[]{:S(2)}) collective-permute-start(f32[128,3584]{1,0:T(8,128)} %fusion.12), channel_id=1, source_target_pairs={{0,1},{1,0},{2,3},{3,2},{8,9},{9,8},{10,11},{11,10},{16,17},{17,16... | collective-permute-start | bytes 5505032 | tf_op jit(solution)/shard_map/ppermute | solution.py:18
  30.5 23.6 %collective-permute-start.7 = (f32[64,3584]{1,0:T(8,128)}, f32[64,3584]{1,0:T(8,128)}, u32[]{:S(2)}, u32[]{:S(2)}) collective-permute-start(f32[64,3584]{1,0:T(8,128)} %slice_add_fusion.7), channel_id=1, source_target_pairs={{0,2},{1,3},{2,0},{3,1},{8,10},{9,11},{10,8},{11,9},{16,18},{17,19... | collective-permute-start | bytes 2752520 | tf_op jit(solution)/shard_map/ppermute | solution.py:18
  32.7 28.3 %collective-permute-start.9 = (f32[64,3584]{1,0:T(8,128)}, f32[64,3584]{1,0:T(8,128)S(1)}, u32[]{:S(2)}, u32[]{:S(2)}) collective-permute-start(f32[64,3584]{1,0:T(8,128)} %slice_add_fusion.6), channel_id=1, source_target_pairs={{0,8},{1,9},{2,10},{3,11},{8,0},{9,1},{10,2},{11,3},{16,24},{17,25... | collective-permute-start | bytes 2752520 | tf_op jit(solution)/shard_map/ppermute | solution.py:18
  36.7 64.4 %collective-permute-start.14 = (f32[64,3584]{1,0:T(8,128)}, f32[64,3584]{1,0:T(8,128)S(1)}, u32[]{:S(2)}, u32[]{:S(2)}) collective-permute-start(f32[64,3584]{1,0:T(8,128)} %slice_add_fusion.4), channel_id=1, source_target_pairs={{0,2},{1,3},{2,0},{3,1},{8,10},{9,11},{10,8},{11,9},{16,18},{17,19... | collective-permute-start | bytes 2752520 | tf_op jit(solution)/shard_map/ppermute | solution.py:18
  54.1 39.2 %collective-permute-start.11 = (f32[64,3584]{1,0:T(8,128)}, f32[64,3584]{1,0:T(8,128)S(1)}, u32[]{:S(2)}, u32[]{:S(2)}) collective-permute-start(f32[64,3584]{1,0:T(8,128)} %slice_add_fusion.5), channel_id=1, source_target_pairs={{0,2},{1,3},{2,0},{3,1},{8,10},{9,11},{10,8},{11,9},{16,18},{17,19... | collective-permute-start | bytes 2752520 | tf_op jit(solution)/shard_map/ppermute | solution.py:18
  57.8 37.9 %collective-permute-start.12 = (f32[64,3584]{1,0:T(8,128)S(1)}, f32[64,3584]{1,0:T(8,128)S(1)}, u32[]{:S(2)}, u32[]{:S(2)}) collective-permute-start(f32[64,3584]{1,0:T(8,128)S(1)} %slice_add_fusion.2), channel_id=1, source_target_pairs={{0,8},{1,9},{2,10},{3,11},{8,0},{9,1},{10,2},{11,3},{16,24},{17,25... | collective-permute-start | bytes 2752520 | tf_op jit(solution)/shard_map/ppermute | solution.py:18
  60.9 38.3 %collective-permute-start.13 = (f32[32,3584]{1,0:T(8,128)S(1)}, f32[32,3584]{1,0:T(8,128)S(1)}, u32[]{:S(2)}, u32[]{:S(2)}) collective-permute-start(f32[32,3584]{1,0:T(8,128)S(1)} %slice_add_fusion.22), channel_id=1, source_target_pairs={{0,8},{1,9},{2,10},{3,11},{8,0},{9,1},{10,2},{11,3},{16,24},{17,25... | collective-permute-start | bytes 1376264 | tf_op jit(solution)/shard_map/ppermute | solution.py:18
  61.8 110.8 %collective-permute-start.24 = (f32[32,3584]{1,0:T(8,128)S(1)}, f32[32,3584]{1,0:T(8,128)S(1)}, u32[]{:S(2)}, u32[]{:S(2)}) collective-permute-start(f32[32,3584]{1,0:T(8,128)S(1)} %slice_add_fusion.20), channel_id=1, source_target_pairs={{0,2},{1,3},{2,0},{3,1},{8,10},{9,11},{10,8},{11,9},{16,18},{17,19... | collective-permute-start | bytes 1376264 | tf_op jit(solution)/shard_map/ppermute | solution.py:18
  93.6 15.9 %collective-permute-start.15 = (f32[32,3584]{1,0:T(8,128)S(1)}, f32[32,3584]{1,0:T(8,128)S(1)}, u32[]{:S(2)}, u32[]{:S(2)}) collective-permute-start(f32[32,3584]{1,0:T(8,128)S(1)} %slice_add_fusion.18), channel_id=1, source_target_pairs={{0,8},{1,9},{2,10},{3,11},{8,0},{9,1},{10,2},{11,3},{16,24},{17,25... | collective-permute-start | bytes 1376264 | tf_op jit(solution)/shard_map/ppermute | solution.py:18
  95.7 102.1 %collective-permute-start.28 = (f32[64,3584]{1,0:T(8,128)S(1)}, f32[64,3584]{1,0:T(8,128)S(1)}, u32[]{:S(2)}, u32[]{:S(2)}) collective-permute-start(f32[64,3584]{1,0:T(8,128)S(1)} %slice_add_fusion), channel_id=1, source_target_pairs={{0,2},{1,3},{2,0},{3,1},{8,10},{9,11},{10,8},{11,9},{16,18},{17,19... | collective-permute-start | bytes 2752520 | tf_op jit(solution)/shard_map/ppermute | solution.py:18
  99.3 43.2 %collective-permute-start.18 = (f32[64,3584]{1,0:T(8,128)S(1)}, f32[64,3584]{1,0:T(8,128)S(1)}, u32[]{:S(2)}, u32[]{:S(2)}) collective-permute-start(f32[64,3584]{1,0:T(8,128)S(1)} %slice_add_fusion.3), channel_id=1, source_target_pairs={{0,2},{1,3},{2,0},{3,1},{8,10},{9,11},{10,8},{11,9},{16,18},{17,19... | collective-permute-start | bytes 2752520 | tf_op jit(solution)/shard_map/ppermute | solution.py:18
  109.7 52.4 %collective-permute-start.22 = (f32[64,3584]{1,0:T(8,128)S(1)}, f32[64,3584]{1,0:T(8,128)S(1)}, u32[]{:S(2)}, u32[]{:S(2)}) collective-permute-start(f32[64,3584]{1,0:T(8,128)S(1)} %slice_add_fusion.1), channel_id=1, source_target_pairs={{0,2},{1,3},{2,0},{3,1},{8,10},{9,11},{10,8},{11,9},{16,18},{17,19... | collective-permute-start | bytes 2752520 | tf_op jit(solution)/shard_map/ppermute | solution.py:18
  120.4 26.4 %collective-permute-start.19 = (f32[16,3584]{1,0:T(8,128)S(1)}, f32[16,3584]{1,0:T(8,128)S(1)}, u32[]{:S(2)}, u32[]{:S(2)}) collective-permute-start(f32[16,3584]{1,0:T(8,128)S(1)} %slice_add_fusion.66), channel_id=1, source_target_pairs={{0,16},{1,17},{2,18},{3,19},{8,24},{9,25},{10,26},{11,27},{16,0},{... | collective-permute-start | bytes 688136 | tf_op jit(solution)/shard_map/ppermute | solution.py:18
  147.1 12.2 %collective-permute-start.21 = (f32[32,3584]{1,0:T(8,128)S(1)}, f32[32,3584]{1,0:T(8,128)S(1)}, u32[]{:S(2)}, u32[]{:S(2)}) collective-permute-start(f32[32,3584]{1,0:T(8,128)S(1)} %slice_add_fusion.12), channel_id=1, source_target_pairs={{0,8},{1,9},{2,10},{3,11},{8,0},{9,1},{10,2},{11,3},{16,24},{17,25... | collective-permute-start | bytes 1376264 | tf_op jit(solution)/shard_map/ppermute | solution.py:18
  151.7 51.6 %collective-permute-start.29 = (f32[32,3584]{1,0:T(8,128)}, f32[32,3584]{1,0:T(8,128)}, u32[]{:S(2)}, u32[]{:S(2)}) collective-permute-start(f32[32,3584]{1,0:T(8,128)} %slice_add_fusion.16), channel_id=1, source_target_pairs={{0,2},{1,3},{2,0},{3,1},{8,10},{9,11},{10,8},{11,9},{16,18},{17,19... | collective-permute-start | bytes 1376264 | tf_op jit(solution)/shard_map/ppermute | solution.py:18
  163.4 15.2 %collective-permute-start.25 = (f32[32,3584]{1,0:T(8,128)S(1)}, f32[32,3584]{1,0:T(8,128)S(1)}, u32[]{:S(2)}, u32[]{:S(2)}) collective-permute-start(f32[32,3584]{1,0:T(8,128)S(1)} %slice_add_fusion.10), channel_id=1, source_target_pairs={{0,8},{1,9},{2,10},{3,11},{8,0},{9,1},{10,2},{11,3},{16,24},{17,25... | collective-permute-start | bytes 1376264 | tf_op jit(solution)/shard_map/ppermute | solution.py:18
  173.5 18.2 %collective-permute-start.26 = (f32[16,3584]{1,0:T(8,128)S(1)}, f32[16,3584]{1,0:T(8,128)S(1)}, u32[]{:S(2)}, u32[]{:S(2)}) collective-permute-start(f32[16,3584]{1,0:T(8,128)S(1)} %slice_add_fusion.45), channel_id=1, source_target_pairs={{0,16},{1,17},{2,18},{3,19},{8,24},{9,25},{10,26},{11,27},{16,0},{... | collective-permute-start | bytes 688136 | tf_op jit(solution)/shard_map/ppermute | solution.py:18
  179.8 16.1 %collective-permute-start.27 = (f32[16,3584]{1,0:T(8,128)S(1)}, f32[16,3584]{1,0:T(8,128)S(1)}, u32[]{:S(2)}, u32[]{:S(2)}) collective-permute-start(f32[16,3584]{1,0:T(8,128)S(1)} %slice_add_fusion.42), channel_id=1, source_target_pairs={{0,16},{1,17},{2,18},{3,19},{8,24},{9,25},{10,26},{11,27},{16,0},{... | collective-permute-start | bytes 688136 | tf_op jit(solution)/shard_map/ppermute | solution.py:18
  200.1 16.8 %collective-permute-start.30 = (f32[32,3584]{1,0:T(8,128)}, f32[32,3584]{1,0:T(8,128)S(1)}, u32[]{:S(2)}, u32[]{:S(2)}) collective-permute-start(f32[32,3584]{1,0:T(8,128)} %slice_add_fusion.8), channel_id=1, source_target_pairs={{0,8},{1,9},{2,10},{3,11},{8,0},{9,1},{10,2},{11,3},{16,24},{17,25... | collective-permute-start | bytes 1376264 | tf_op jit(solution)/shard_map/ppermute | solution.py:18
  204.9 13.7 %collective-permute-start.31 = (f32[16,3584]{1,0:T(8,128)S(1)}, f32[16,3584]{1,0:T(8,128)S(1)}, u32[]{:S(2)}, u32[]{:S(2)}) collective-permute-start(f32[16,3584]{1,0:T(8,128)S(1)} %slice_add_fusion.33), channel_id=1, source_target_pairs={{0,16},{1,17},{2,18},{3,19},{8,24},{9,25},{10,26},{11,27},{16,0},{... | collective-permute-start | bytes 688136 | tf_op jit(solution)/shard_map/ppermute | solution.py:18
  218.5 11.2 %collective-permute-start.32 = (f32[16,3584]{1,0:T(8,128)S(1)}, f32[16,3584]{1,0:T(8,128)S(1)}, u32[]{:S(2)}, u32[]{:S(2)}) collective-permute-start(f32[16,3584]{1,0:T(8,128)S(1)} %slice_add_fusion.30), channel_id=1, source_target_pairs={{0,16},{1,17},{2,18},{3,19},{8,24},{9,25},{10,26},{11,27},{16,0},{... | collective-permute-start | bytes 688136 | tf_op jit(solution)/shard_map/ppermute | solution.py:18
  (35 other events, 665.9 us)

commit v2 on v1

--- a/solution.py
+++ b/solution.py
@@ -5,7 +5,8 @@
 
 
 GROUP = ("dp", "shard")
-CHUNKS = 4
+FIRST, LATER = (16, 28, 28, 24, 16), (24, 16, 24, 28, 20)
+EARLY = (1,)
 step_size = 0.5
 clip_level = 1.0
 
@@ -55,10 +56,11 @@
             now = arrival[job]
         order, width = jobs[job]
         at = stage[job]
-        now += 2.5
+        now += 3.6 if at == len(order) else 2.7 if at else 2.2
         if at < len(order):
             link = links[order[at]]
-            rate = 6e5 if link == "core" else 5e4
+            far = link == "dp" and at == len(order) - 1
+            rate = 6e5 if link == "core" else 2.6e4 if far else 5.15e4
             sent = (size >> (at + 1)) * own_rows * width * 4 / rate
             free[link] = max(free.get(link, 0.0), now) + sent
             arrival[job] = free[link] + 2.0
@@ -112,8 +114,14 @@
 
 
 def all_jobs(layers, columns, plain, early):
-    width = columns // CHUNKS
-    return [(early if chunk == 1 else plain, width) for _ in range(layers) for chunk in range(CHUNKS)]
+    jobs = []
+    for layer in range(layers):
+        shares = FIRST if layer == 0 else LATER
+        unit = columns // sum(shares)
+        for chunk, share in enumerate(shares):
+            is_early = layer == 0 and chunk in EARLY
+            jobs.append((layer, unit * sum(shares[:chunk]), early if is_early else plain, unit * share))
+    return jobs
 
 
 def on_device(activations, out_grads, weights, shadow, counts):
@@ -123,23 +131,21 @@
     size = lax.axis_size(GROUP)
     me = lax.axis_index(GROUP)
     links, plain, early = exchange_order(lax.axis_size("dp"), lax.axis_size("shard"))
-    jobs = all_jobs(layers, columns, plain, early)
+    plan = all_jobs(layers, columns, plain, early)
+    jobs = [job[2:] for job in plan]
     own_slot = (jnp.arange(experts) == lax.axis_index("expert")).astype(jnp.float32)
     load_sums = summed_over(counts[:, 0, :].astype(jnp.float32), "expert")
 
-    width = columns // CHUNKS
     lefts, rights = [], []
-    for layer in range(layers):
-        inputs = activations[layer, 0]
-        rows_of = {}
-        for order in (plain, early):
-            rows_of[tuple(order)] = relative_rows(inputs, order, own_rows, me)
-        for chunk in range(CHUNKS):
-            order = early if chunk == 1 else plain
-            lefts.append(rows_of[tuple(order)])
-            rights.append(out_grads[layer, 0, :, chunk * width : (chunk + 1) * width])
+    rows_of = {}
+    for layer, begin, order, width in plan:
+        key = (layer, tuple(order))
+        if key not in rows_of:
+            rows_of[key] = relative_rows(activations[layer, 0], order, own_rows, me)
+        lefts.append(rows_of[key])
+        rights.append(out_grads[layer, 0, :, begin : begin + width])
     pieces = reduce_all(jobs, links, lefts, rights, own_rows, size)
-    grads = [pieces[layer * CHUNKS : (layer + 1) * CHUNKS] for layer in range(layers)]
+    grads = [[p for p, job in zip(pieces, plan) if job[0] == layer] for layer in range(layers)]
     squares = jnp.stack([sum(jnp.sum(piece * piece) for piece in layer) for layer in grads])
     totals = jnp.concatenate([load_sums.reshape(-1), squares])
     for axis in ("shard", "dp"):
@@ -147,16 +153,14 @@
     load_totals = totals[: layers * experts].reshape(layers, experts)
     total_squares = totals[layers * experts :]
 
+    own_load = jnp.sum(load_totals * own_slot, axis=1)
+    mean_load = jnp.mean(load_totals, axis=1)
+    root_mean = jnp.sqrt(total_squares / (own_rows * size * columns))
+    factors = step_size * (own_load / mean_load) * clip_level / jnp.maximum(root_mean, clip_level)
+    betas = own_load / (own_load + mean_load)
     all_weights, all_shadow = [], []
     for layer in range(layers):
-        loads = load_totals[layer]
-        own_load = jnp.sum(loads * own_slot)
-        mean_load = jnp.mean(loads)
-        root_mean = jnp.sqrt(total_squares[layer] / (own_rows * size * columns))
-        factor = (
-            step_size * (own_load / mean_load) * clip_level / jnp.maximum(root_mean, clip_level)
-        )
-        beta = own_load / (own_load + mean_load)
+        factor, beta = factors[layer], betas[layer]
         summed = jnp.concatenate(grads[layer], axis=1)
         updated = weights[layer, 0] - factor * summed
         previous = shadow[layer, 0]

time: 260 us -> 239 us (0.919)
  waiting for transfers between devices: 139 us -> 95.6 us
  starting transfers between devices: 39.6 us -> 55.4 us
  matrix products: 54.1 us -> 60.3 us
  between operations: 12.8 us -> 7.51 us
  local copies, waits for them, and re-layouts: 1.53 us -> 5.66 us
    ppermute x32 -> x40, waiting for transfers between devices: 126 us -> 83.6 us  [swap(): return lax.ppermute(value, GROUP, [(g, g ^ bit) for g in range(size)])]
    ppermute x32 -> x40, starting transfers between devices: 34.9 us -> 51.1 us  [swap(): return lax.ppermute(value, GROUP, [(g, g ^ bit) for g in range(size)])]
    dot_general x40 -> x50, matrix products: 50.3 us -> 56.9 us  [reduce_all(): lax.dot_general(left[low:high], rights[job], (((1,), (0,)), ((), ())), pr...]
    unnamed x44 -> x58, local copies, waits for them, and re-layouts: 0.8 us -> 3.64 us
    reduce_sum x7 -> x9, other arithmetic: 5.72 us -> 6.3 us  [on_device(): jnp.sum(piece * piece)]
  transfers between devices with their start and end apart: 37 -> 45, of which waited for: 22 -> 24; matrix products, arithmetic and copies ran while one was open for 19% -> 25% of each run, Pallas kernels for 0% -> 0%
where the time goes in v2:
time: 239 us; the launch traced here: 238 us
  waiting for transfers between devices  95.6 us (40%)
  matrix products  60.3 us (25%)
  starting transfers between devices  55.4 us (23%)
  other arithmetic  14 us (6%)
  between operations  7.51 us (3%)
  local copies, waits for them, and re-layouts  5.66 us (2%)
    ppermute x40, waiting for transfers between devices, swap(): return lax.ppermute(value, GROUP, [(g, g ^ bit) for g in range(size)])  83.6 us
    dot_general x50, matrix products, reduce_all(): lax.dot_general(left[low:high], rights[job], (((1,), (0,)), ((), ())), pr...  56.9 us
    ppermute x40, starting transfers between devices, swap(): return lax.ppermute(value, GROUP, [(g, g ^ bit) for g in range(size)])  51.1 us
    ppermute x5, waiting for transfers between devices, summed_over(): lax.ppermute(total, axis, [(g, g ^ bit) for g in range(size)])  12.1 us
    reduce_sum x9, other arithmetic, on_device(): jnp.sum(piece * piece)  6.3 us
  transfers between devices with their start and end apart: 45, of which 24 were waited for; matrix products, arithmetic and copies ran while one was open for 25% of the time, Pallas kernels for 0%

profile of v2, /device:TPU:0, one launch (start us, length us, event | category | flops | bytes accessed | tf_op | source)
XLA Modules:
  0.0 238.5 jit_solution(15878031672724131287)
XLA Ops:
  9.3 3.0 %collective-permute-start.5 = (f32[64,2048]{1,0:T(8,128)S(1)}, f32[64,2048]{1,0:T(8,128)S(1)}, u32[]{:S(2)}, u32[]{:S(2)}) collective-permute-start(f32[64,2048]{1,0:T(8,128)S(1)} %slice_add_fusion.9), channel_id=1, source_target_pairs={{0,2},{1,3},{2,0},{3,1},{8,10},{9,11},{10,8},{11,9},{16,18},{17,19... | collective-permute-start | bytes 1572872 | tf_op jit(solution)/shard_map/ppermute | solution.py:19
  16.6 7.8 %collective-permute-done.5 = f32[64,2048]{1,0:T(8,128)S(1)} collective-permute-done((f32[64,2048]{1,0:T(8,128)S(1)}, f32[64,2048]{1,0:T(8,128)S(1)}, u32[]{:S(2)}, u32[]{:S(2)}) %collective-permute-start.5) | collective-permute-done | bytes 524320 | tf_op jit(solution)/shard_map/ppermute | solution.py:19
  32.0 16.4 %collective-permute-done.8 = f32[64,3584]{1,0:T(8,128)S(1)} collective-permute-done((f32[64,3584]{1,0:T(8,128)S(1)}, f32[64,3584]{1,0:T(8,128)S(1)}, u32[]{:S(2)}, u32[]{:S(2)}) %collective-permute-start.8) | collective-permute-done | bytes 917536 | tf_op jit(solution)/shard_map/ppermute | solution.py:19
  50.6 2.9 %collective-permute-done.10 = f32[32,2048]{1,0:T(8,128)S(1)} collective-permute-done((f32[32,2048]{1,0:T(8,128)S(1)}, f32[32,2048]{1,0:T(8,128)S(1)}, u32[]{:S(2)}, u32[]{:S(2)}) %collective-permute-start.10) | collective-permute-done | bytes 262176 | tf_op jit(solution)/shard_map/ppermute | solution.py:19
  57.1 2.6 %collective-permute-start.12 = (f32[16,2048]{1,0:T(8,128)S(1)}, f32[16,2048]{1,0:T(8,128)S(1)}, u32[]{:S(2)}, u32[]{:S(2)}) collective-permute-start(f32[16,2048]{1,0:T(8,128)S(1)} %slice_add_fusion.87), channel_id=1, source_target_pairs={{0,16},{1,17},{2,18},{3,19},{8,24},{9,25},{10,26},{11,27},{16,0},{... | collective-permute-start | bytes 393224 | tf_op jit(solution)/shard_map/ppermute | solution.py:19
  61.2 4.8 %collective-permute-done.12 = f32[16,2048]{1,0:T(8,128)S(1)} collective-permute-done((f32[16,2048]{1,0:T(8,128)S(1)}, f32[16,2048]{1,0:T(8,128)S(1)}, u32[]{:S(2)}, u32[]{:S(2)}) %collective-permute-start.12) | collective-permute-done | bytes 131104 | tf_op jit(solution)/shard_map/ppermute | solution.py:19
  67.7 7.2 %collective-permute-done.14 = f32[64,3072]{1,0:T(8,128)S(1)} collective-permute-done((f32[64,3072]{1,0:T(8,128)S(1)}, f32[64,3072]{1,0:T(8,128)S(1)}, u32[]{:S(2)}, u32[]{:S(2)}) %collective-permute-start.14) | collective-permute-done | bytes 786464 | tf_op jit(solution)/shard_map/ppermute | solution.py:19
  90.0 8.4 %collective-permute-done.17 = f32[64,2048]{1,0:T(8,128)S(1)} collective-permute-done((f32[64,2048]{1,0:T(8,128)}, f32[64,2048]{1,0:T(8,128)S(1)}, u32[]{:S(2)}, u32[]{:S(2)}) %collective-permute-start.17) | collective-permute-done | bytes 524320 | tf_op jit(solution)/shard_map/ppermute | solution.py:19
  103.3 2.8 %collective-permute-start.20 = (f32[16,3584]{1,0:T(8,128)}, f32[16,3584]{1,0:T(8,128)S(1)}, u32[]{:S(2)}, u32[]{:S(2)}) collective-permute-start(f32[16,3584]{1,0:T(8,128)} %slice_add_fusion.45), channel_id=1, source_target_pairs={{0,16},{1,17},{2,18},{3,19},{8,24},{9,25},{10,26},{11,27},{16,0},{... | collective-permute-start | bytes 688136 | tf_op jit(solution)/shard_map/ppermute | solution.py:19
  106.1 2.4 slice_add_fusion.6
  108.5 4.9 %collective-permute-done.20 = f32[16,3584]{1,0:T(8,128)S(1)} collective-permute-done((f32[16,3584]{1,0:T(8,128)}, f32[16,3584]{1,0:T(8,128)S(1)}, u32[]{:S(2)}, u32[]{:S(2)}) %collective-permute-start.20) | collective-permute-done | bytes 229408 | tf_op jit(solution)/shard_map/ppermute | solution.py:19
  119.8 2.4 %collective-permute-start.24 = (f32[16,3072]{1,0:T(8,128)S(1)}, f32[16,3072]{1,0:T(8,128)S(1)}, u32[]{:S(2)}, u32[]{:S(2)}) collective-permute-start(f32[16,3072]{1,0:T(8,128)S(1)} %slice_add_fusion.63), channel_id=1, source_target_pairs={{0,16},{1,17},{2,18},{3,19},{8,24},{9,25},{10,26},{11,27},{16,0},{... | collective-permute-start | bytes 589832 | tf_op jit(solution)/shard_map/ppermute | solution.py:19
  133.3 6.5 %collective-permute-done.25 = f32[32,3072]{1,0:T(8,128)S(1)} collective-permute-done((f32[32,3072]{1,0:T(8,128)S(1)}, f32[32,3072]{1,0:T(8,128)S(1)}, u32[]{:S(2)}, u32[]{:S(2)}) %collective-permute-start.25) | collective-permute-done | bytes 393248 | tf_op jit(solution)/shard_map/ppermute | solution.py:19
  150.3 2.8 %collective-permute-done.29 = f32[64,3072]{1,0:T(8,128)S(1)} collective-permute-done((f32[64,3072]{1,0:T(8,128)}, f32[64,3072]{1,0:T(8,128)S(1)}, u32[]{:S(2)}, u32[]{:S(2)}) %collective-permute-start.29) | collective-permute-done | bytes 786464 | tf_op jit(solution)/shard_map/ppermute | solution.py:19
  153.1 2.2 slice_add_fusion.16
  168.7 2.8 %collective-permute-start.34 = (f32[16,2048]{1,0:T(8,128)S(1)}, f32[16,2048]{1,0:T(8,128)S(1)}, u32[]{:S(2)}, u32[]{:S(2)}) collective-permute-start(f32[16,2048]{1,0:T(8,128)S(1)} %slice_add_fusion.75), channel_id=1, source_target_pairs={{0,16},{1,17},{2,18},{3,19},{8,24},{9,25},{10,26},{11,27},{16,0},{... | collective-permute-start | bytes 393224 | tf_op jit(solution)/shard_map/ppermute | solution.py:19
  173.8 2.6 %slice_add_fusion.10 = f32[32,3584]{1,0:T(8,128)} fusion(f32[64,3584]{1,0:T(8,128)} %collective-permute-done.33, f32[128,3584]{1,0:T(8,128)} %copy-done.2, bf16[2,1,128,14336]{3,2,1,0:T(8,128)(2,1)} %param.6, bf16[256,128]{1,0:T(8,128)(2,1)S(1)} %convolution_convert_fusion.2), kind=kOutput, calls=%fused_computation.142 | convolution fusion | flops 29589504 | bytes 2301952 | tf_op jit(solution)/shard_map/dot_general | solution.py:92
  187.1 2.2 slice_add_fusion.22
  189.3 2.5 %collective-permute-start.38 = (f32[32,2560]{1,0:T(8,128)}, f32[32,2560]{1,0:T(8,128)S(1)}, u32[]{:S(2)}, u32[]{:S(2)}) collective-permute-start(f32[32,2560]{1,0:T(8,128)} %slice_add_fusion.22), channel_id=1, source_target_pairs={{0,8},{1,9},{2,10},{3,11},{8,0},{9,1},{10,2},{11,3},{16,24},{17,25... | collective-permute-start | bytes 983048 | tf_op jit(solution)/shard_map/ppermute | solution.py:19
  197.0 4.8 %collective-permute-done.38 = f32[32,2560]{1,0:T(8,128)S(1)} collective-permute-done((f32[32,2560]{1,0:T(8,128)}, f32[32,2560]{1,0:T(8,128)S(1)}, u32[]{:S(2)}, u32[]{:S(2)}) %collective-permute-start.38) | collective-permute-done | bytes 327712 | tf_op jit(solution)/shard_map/ppermute | solution.py:19
  204.6 6.4 %collective-permute-done.39 = f32[16,3584]{1,0:T(8,128)S(1)} collective-permute-done((f32[16,3584]{1,0:T(8,128)S(1)}, f32[16,3584]{1,0:T(8,128)S(1)}, u32[]{:S(2)}, u32[]{:S(2)}) %collective-permute-start.39) | collective-permute-done | bytes 229408 | tf_op jit(solution)/shard_map/ppermute | solution.py:19
  221.6 3.6 %collective-permute-done.43 = f32[6]{0:T(128)S(1)} collective-permute-done((f32[6]{0:T(128)S(1)}, f32[6]{0:T(128)S(1)}, u32[]{:S(2)}, u32[]{:S(2)}) %collective-permute-start.43) | collective-permute-done | bytes 56 | tf_op jit(solution)/shard_map/ppermute | solution.py:26
  225.9 3.8 %collective-permute-done.44 = f32[6]{0:T(128)S(1)} collective-permute-done((f32[6]{0:T(128)S(1)}, f32[6]{0:T(128)S(1)}, u32[]{:S(2)}, u32[]{:S(2)}) %collective-permute-start.44) | collective-permute-done | bytes 56 | tf_op jit(solution)/shard_map/ppermute | solution.py:26
  231.2 4.6 %bitcast_add_fusion.1 = (f32[1,16,14336]{2,1,0:T(8,128)S(1)}, f32[1,16,14336]{2,1,0:T(8,128)S(1)}, f32[1,16,14336]{2,1,0:T(8,128)S(1)}, f32[1,16,14336]{2,1,0:T(8,128)S(1)}) fusion(f32[2,1,16,14336]{3,2,1,0:T(8,128)S(1)} %copy-done.1, f32[]{:T(128)} %bitcast.32, f32[1,16,14336]{2,1,0:T(8,128)} %bitcast_dynamic-update-slice_fusion.8, f32[]{:T(128)} %bitcast.16, ...), kind=kLoop, calls=%fused_computation.11 | loop fusion | flops 2293760 | bytes 9175056 | tf_op jit(solution)/shard_map/add | solution.py:168
  (209 shorter events, 120.4 us)
Async XLA Ops:
  9.3 15.2 %collective-permute-start.5 = (f32[64,2048]{1,0:T(8,128)S(1)}, f32[64,2048]{1,0:T(8,128)S(1)}, u32[]{:S(2)}, u32[]{:S(2)}) collective-permute-start(f32[64,2048]{1,0:T(8,128)S(1)} %slice_add_fusion.9), channel_id=1, source_target_pairs={{0,2},{1,3},{2,0},{3,1},{8,10},{9,11},{10,8},{11,9},{16,18},{17,19... | collective-permute-start | bytes 1572872 | tf_op jit(solution)/shard_map/ppermute | solution.py:19
  25.1 23.3 %collective-permute-start.8 = (f32[64,3584]{1,0:T(8,128)S(1)}, f32[64,3584]{1,0:T(8,128)S(1)}, u32[]{:S(2)}, u32[]{:S(2)}) collective-permute-start(f32[64,3584]{1,0:T(8,128)S(1)} %slice_add_fusion.2), channel_id=1, source_target_pairs={{0,8},{1,9},{2,10},{3,11},{8,0},{9,1},{10,2},{11,3},{16,24},{17,25... | collective-permute-start | bytes 2752520 | tf_op jit(solution)/shard_map/ppermute | solution.py:19
  28.4 21.1 %collective-permute-start.9 = (f32[128,2048]{1,0:T(8,128)S(1)}, f32[128,2048]{1,0:T(8,128)S(1)}, u32[]{:S(2)}, u32[]{:S(2)}) collective-permute-start(f32[128,2048]{1,0:T(8,128)S(1)} %fusion.94), channel_id=1, source_target_pairs={{0,1},{1,0},{2,3},{3,2},{8,9},{9,8},{10,11},{11,10},{16,17},{17,16... | collective-permute-start | bytes 3145736 | tf_op jit(solution)/shard_map/ppermute | solution.py:19
  28.6 25.1 %collective-permute-start.11 = (f32[64,3584]{1,0:T(8,128)S(1)}, f32[64,3584]{1,0:T(8,128)S(1)}, u32[]{:S(2)}, u32[]{:S(2)}) collective-permute-start(f32[64,3584]{1,0:T(8,128)S(1)} %slice_add_fusion.1), channel_id=1, source_target_pairs={{0,2},{1,3},{2,0},{3,1},{8,10},{9,11},{10,8},{11,9},{16,18},{17,19... | collective-permute-start | bytes 2752520 | tf_op jit(solution)/shard_map/ppermute | solution.py:19
  30.1 23.4 %collective-permute-start.10 = (f32[32,2048]{1,0:T(8,128)S(1)}, f32[32,2048]{1,0:T(8,128)S(1)}, u32[]{:S(2)}, u32[]{:S(2)}) collective-permute-start(f32[32,2048]{1,0:T(8,128)S(1)} %slice_add_fusion.28), channel_id=1, source_target_pairs={{0,8},{1,9},{2,10},{3,11},{8,0},{9,1},{10,2},{11,3},{16,24},{17,25... | collective-permute-start | bytes 786440 | tf_op jit(solution)/shard_map/ppermute | solution.py:19
  54.8 21.1 %collective-permute-start.15 = (f32[128,3584]{1,0:T(8,128)S(1)}, f32[128,3584]{1,0:T(8,128)S(1)}, u32[]{:S(2)}, u32[]{:S(2)}) collective-permute-start(f32[128,3584]{1,0:T(8,128)S(1)} %fusion.10), channel_id=1, source_target_pairs={{0,1},{1,0},{2,3},{3,2},{8,9},{9,8},{10,11},{11,10},{16,17},{17,16... | collective-permute-start | bytes 5505032 | tf_op jit(solution)/shard_map/ppermute | solution.py:19
  55.4 19.5 %collective-permute-start.14 = (f32[64,3072]{1,0:T(8,128)S(1)}, f32[64,3072]{1,0:T(8,128)S(1)}, u32[]{:S(2)}, u32[]{:S(2)}) collective-permute-start(f32[64,3072]{1,0:T(8,128)S(1)} %slice_add_fusion.5), channel_id=1, source_target_pairs={{0,2},{1,3},{2,0},{3,1},{8,10},{9,11},{10,8},{11,9},{16,18},{17,19... | collective-permute-start | bytes 2359304 | tf_op jit(solution)/shard_map/ppermute | solution.py:19
  59.7 17.5 %collective-permute-start.16 = (f32[32,3584]{1,0:T(8,128)S(1)}, f32[32,3584]{1,0:T(8,128)S(1)}, u32[]{:S(2)}, u32[]{:S(2)}) collective-permute-start(f32[32,3584]{1,0:T(8,128)S(1)} %slice_add_fusion.12), channel_id=1, source_target_pairs={{0,8},{1,9},{2,10},{3,11},{8,0},{9,1},{10,2},{11,3},{16,24},{17,25... | collective-permute-start | bytes 1376264 | tf_op jit(solution)/shard_map/ppermute | solution.py:19
  79.6 23.7 %collective-permute-start.19 = (f32[128,2560]{1,0:T(8,128)}, f32[128,2560]{1,0:T(8,128)}, u32[]{:S(2)}, u32[]{:S(2)}) collective-permute-start(f32[128,2560]{1,0:T(8,128)} %fusion.82), channel_id=1, source_target_pairs={{0,1},{1,0},{2,3},{3,2},{8,9},{9,8},{10,11},{11,10},{16,17},{17,16... | collective-permute-start | bytes 3932168 | tf_op jit(solution)/shard_map/ppermute | solution.py:19
  83.4 15.0 %collective-permute-start.17 = (f32[64,2048]{1,0:T(8,128)}, f32[64,2048]{1,0:T(8,128)S(1)}, u32[]{:S(2)}, u32[]{:S(2)}) collective-permute-start(f32[64,2048]{1,0:T(8,128)} %slice_add_fusion.8), channel_id=1, source_target_pairs={{0,2},{1,3},{2,0},{3,1},{8,10},{9,11},{10,8},{11,9},{16,18},{17,19... | collective-permute-start | bytes 1572872 | tf_op jit(solution)/shard_map/ppermute | solution.py:19
  85.0 30.7 %collective-permute-start.21 = (f32[64,3072]{1,0:T(8,128)}, f32[64,3072]{1,0:T(8,128)S(1)}, u32[]{:S(2)}, u32[]{:S(2)}) collective-permute-start(f32[64,3072]{1,0:T(8,128)} %slice_add_fusion.4), channel_id=1, source_target_pairs={{0,2},{1,3},{2,0},{3,1},{8,10},{9,11},{10,8},{11,9},{16,18},{17,19... | collective-permute-start | bytes 2359304 | tf_op jit(solution)/shard_map/ppermute | solution.py:19
  85.4 39.7 %collective-permute-start.23 = (f32[32,3584]{1,0:T(8,128)}, f32[32,3584]{1,0:T(8,128)S(1)}, u32[]{:S(2)}, u32[]{:S(2)}) collective-permute-start(f32[32,3584]{1,0:T(8,128)} %slice_add_fusion.14), channel_id=1, source_target_pairs={{0,2},{1,3},{2,0},{3,1},{8,10},{9,11},{10,8},{11,9},{16,18},{17,19... | collective-permute-start | bytes 1376264 | tf_op jit(solution)/shard_map/ppermute | solution.py:19
  87.1 14.3 %collective-permute-start.18 = (f32[32,3072]{1,0:T(8,128)}, f32[32,3072]{1,0:T(8,128)S(1)}, u32[]{:S(2)}, u32[]{:S(2)}) collective-permute-start(f32[32,3072]{1,0:T(8,128)} %slice_add_fusion.20), channel_id=1, source_target_pairs={{0,8},{1,9},{2,10},{3,11},{8,0},{9,1},{10,2},{11,3},{16,24},{17,25... | collective-permute-start | bytes 1179656 | tf_op jit(solution)/shard_map/ppermute | solution.py:19
  98.4 44.3 %collective-permute-start.26 = (f32[64,2048]{1,0:T(8,128)}, f32[64,2048]{1,0:T(8,128)S(1)}, u32[]{:S(2)}, u32[]{:S(2)}) collective-permute-start(f32[64,2048]{1,0:T(8,128)} %slice_add_fusion.7), channel_id=1, source_target_pairs={{0,2},{1,3},{2,0},{3,1},{8,10},{9,11},{10,8},{11,9},{16,18},{17,19... | collective-permute-start | bytes 1572872 | tf_op jit(solution)/shard_map/ppermute | solution.py:19
  101.4 51.8 %collective-permute-start.29 = (f32[64,3072]{1,0:T(8,128)}, f32[64,3072]{1,0:T(8,128)S(1)}, u32[]{:S(2)}, u32[]{:S(2)}) collective-permute-start(f32[64,3072]{1,0:T(8,128)} %slice_add_fusion.3), channel_id=1, source_target_pairs={{0,2},{1,3},{2,0},{3,1},{8,10},{9,11},{10,8},{11,9},{16,18},{17,19... | collective-permute-start | bytes 2359304 | tf_op jit(solution)/shard_map/ppermute | solution.py:19
  115.8 58.0 %collective-permute-start.33 = (f32[64,3584]{1,0:T(8,128)}, f32[64,3584]{1,0:T(8,128)}, u32[]{:S(2)}, u32[]{:S(2)}) collective-permute-start(f32[64,3584]{1,0:T(8,128)} %slice_add_fusion), channel_id=1, source_target_pairs={{0,2},{1,3},{2,0},{3,1},{8,10},{9,11},{10,8},{11,9},{16,18},{17,19... | collective-permute-start | bytes 2752520 | tf_op jit(solution)/shard_map/ppermute | solution.py:19
  125.1 14.7 %collective-permute-start.25 = (f32[32,3072]{1,0:T(8,128)S(1)}, f32[32,3072]{1,0:T(8,128)S(1)}, u32[]{:S(2)}, u32[]{:S(2)}) collective-permute-start(f32[32,3072]{1,0:T(8,128)S(1)} %slice_add_fusion.18), channel_id=1, source_target_pairs={{0,8},{1,9},{2,10},{3,11},{8,0},{9,1},{10,2},{11,3},{16,24},{17,25... | collective-permute-start | bytes 1179656 | tf_op jit(solution)/shard_map/ppermute | solution.py:19
  129.9 19.2 %collective-permute-start.28 = (f32[16,3584]{1,0:T(8,128)S(1)}, f32[16,3584]{1,0:T(8,128)S(1)}, u32[]{:S(2)}, u32[]{:S(2)}) collective-permute-start(f32[16,3584]{1,0:T(8,128)S(1)} %slice_add_fusion.39), channel_id=1, source_target_pairs={{0,16},{1,17},{2,18},{3,19},{8,24},{9,25},{10,26},{11,27},{16,0},{... | collective-permute-start | bytes 688136 | tf_op jit(solution)/shard_map/ppermute | solution.py:19
  142.7 44.4 %collective-permute-start.36 = (f32[64,2560]{1,0:T(8,128)}, f32[64,2560]{1,0:T(8,128)}, u32[]{:S(2)}, u32[]{:S(2)}) collective-permute-start(f32[64,2560]{1,0:T(8,128)} %slice_add_fusion.6), channel_id=1, source_target_pairs={{0,2},{1,3},{2,0},{3,1},{8,10},{9,11},{10,8},{11,9},{16,18},{17,19... | collective-permute-start | bytes 1966088 | tf_op jit(solution)/shard_map/ppermute | solution.py:19
  147.1 17.9 %collective-permute-start.30 = (f32[16,3072]{1,0:T(8,128)}, f32[16,3072]{1,0:T(8,128)}, u32[]{:S(2)}, u32[]{:S(2)}) collective-permute-start(f32[16,3072]{1,0:T(8,128)} %slice_add_fusion.57), channel_id=1, source_target_pairs={{0,16},{1,17},{2,18},{3,19},{8,24},{9,25},{10,26},{11,27},{16,0},{... | collective-permute-start | bytes 589832 | tf_op jit(solution)/shard_map/ppermute | solution.py:19
  157.1 14.4 %collective-permute-start.32 = (f32[32,3072]{1,0:T(8,128)}, f32[32,3072]{1,0:T(8,128)S(1)}, u32[]{:S(2)}, u32[]{:S(2)}) collective-permute-start(f32[32,3072]{1,0:T(8,128)} %slice_add_fusion.16), channel_id=1, source_target_pairs={{0,8},{1,9},{2,10},{3,11},{8,0},{9,1},{10,2},{11,3},{16,24},{17,25... | collective-permute-start | bytes 1179656 | tf_op jit(solution)/shard_map/ppermute | solution.py:19
  179.6 14.8 %collective-permute-start.37 = (f32[32,3584]{1,0:T(8,128)}, f32[32,3584]{1,0:T(8,128)}, u32[]{:S(2)}, u32[]{:S(2)}) collective-permute-start(f32[32,3584]{1,0:T(8,128)} %slice_add_fusion.10), channel_id=1, source_target_pairs={{0,8},{1,9},{2,10},{3,11},{8,0},{9,1},{10,2},{11,3},{16,24},{17,25... | collective-permute-start | bytes 1376264 | tf_op jit(solution)/shard_map/ppermute | solution.py:19
  189.3 12.4 %collective-permute-start.38 = (f32[32,2560]{1,0:T(8,128)}, f32[32,2560]{1,0:T(8,128)S(1)}, u32[]{:S(2)}, u32[]{:S(2)}) collective-permute-start(f32[32,2560]{1,0:T(8,128)} %slice_add_fusion.22), channel_id=1, source_target_pairs={{0,8},{1,9},{2,10},{3,11},{8,0},{9,1},{10,2},{11,3},{16,24},{17,25... | collective-permute-start | bytes 983048 | tf_op jit(solution)/shard_map/ppermute | solution.py:19
  196.1 15.0 %collective-permute-start.39 = (f32[16,3584]{1,0:T(8,128)S(1)}, f32[16,3584]{1,0:T(8,128)S(1)}, u32[]{:S(2)}, u32[]{:S(2)}) collective-permute-start(f32[16,3584]{1,0:T(8,128)S(1)} %slice_add_fusion.33), channel_id=1, source_target_pairs={{0,16},{1,17},{2,18},{3,19},{8,24},{9,25},{10,26},{11,27},{16,0},{... | collective-permute-start | bytes 688136 | tf_op jit(solution)/shard_map/ppermute | solution.py:19
  (46 other events, 708.4 us)
